TPU v7x, 32 devices: a whole 2x2x4 slice. The times are simulated.
32 devices in a mesh: query: 4 (over y, x), train: 4 (over z), mp: 2 (over core).
Axes of the slice: x: 2, y: 2, z: 4, core: 2. Of those that a mesh axis runs over, the one named last changes fastest.
Arguments:
- residual: bfloat16 [512, 8192], P('train'), may hold values from -6 to 6
- norm_gain: float32 [8192], replicated, may hold values from 0.1 to 1.9
- gate_weight: bfloat16 [8192, 14336], P('train', ('query', 'mp')), may hold values from -0.0625 to 0.0625
- up_weight: bfloat16 [8192, 14336], P('train', ('query', 'mp')), may hold values from -0.0625 to 0.0625
- out_grad: bfloat16 [512, 8192], P('train', ('query', 'mp')), may hold values from -6 to 6
- left_factor: bfloat16 [8, 32, 14336], P(('query', 'mp')), may hold values from -0.0078125 to 0.0078125
- right_factor: bfloat16 [8, 32, 8192], P(('query', 'mp')), may hold values from -0.0625 to 0.0625
Outputs:
- scores: float32 [8, 512], P(('query', 'mp'), 'train')
All inputs are finite; a program needn't handle non-finite values.
Results may differ from a plain program's by a relative error of at most 0.023.
Values may be sent and summed in bfloat16 or wider, within the bound.
A program may use at most 64 MiB of HBM per device.

v0:
```python
import jax
import jax.numpy as jnp
from jax import lax
from jax.sharding import PartitionSpec as P

norm_eps = 1e-05


def on_device(residual, norm_gain, gate_weight, up_weight, out_grad, left_factor, right_factor):
    values = residual.astype(jnp.float32)
    mean_sq = jnp.mean(values * values, axis=1, keepdims=True)
    normed = (values * lax.rsqrt(mean_sq + norm_eps) * norm_gain[None, :]).astype(jnp.bfloat16)
    tok_rows = normed.shape[0]
    hidden_cols = gate_weight.shape[1]
    all_rows = lax.all_to_all(normed, "train", split_axis=1, concat_axis=0, tiled=True)
    paired = jnp.concatenate([gate_weight, up_weight], axis=1)
    summed = lax.psum_scatter(
        jnp.dot(all_rows, paired, preferred_element_type=jnp.float32).astype(jnp.bfloat16),
        "train",
        scatter_dimension=0,
        tiled=True,
    ).astype(jnp.float32)
    activation = (jax.nn.silu(summed[:, :hidden_cols]) * summed[:, hidden_cols:]).astype(
        jnp.bfloat16
    )
    queries = left_factor.shape[0]
    factor_rank = left_factor.shape[1]
    contract = (((1,), (1,)), ((), ()))
    left_flat = left_factor.reshape(queries * factor_rank, left_factor.shape[2])
    columns = left_flat
    projected = lax.dot_general(
        columns,
        lax.all_gather(activation, ("query", "mp"), axis=1, tiled=True),
        contract,
        preferred_element_type=jnp.float32,
    )
    right_flat = right_factor.reshape(queries * factor_rank, right_factor.shape[2])
    columns = right_flat
    sensed = lax.dot_general(
        columns,
        lax.all_gather(out_grad, ("query", "mp"), axis=1, tiled=True),
        contract,
        preferred_element_type=jnp.float32,
    )
    return jnp.sum((projected * sensed).reshape(queries, factor_rank, tok_rows), axis=1)


def solution(mesh):
    placed = (
        P("train", None),
        P(),
        P("train", ("query", "mp")),
        P("train", ("query", "mp")),
        P("train", ("query", "mp")),
        P(("query", "mp"), None, None),
        P(("query", "mp"), None, None),
    )
    return jax.shard_map(
        on_device,
        mesh=mesh,
        in_specs=placed,
        out_specs=P(("query", "mp"), "train"),
        check_vma=False,
    )
```

profile of v0, /device:TPU:0, one launch (start us, length us, event | category | flops | bytes accessed | tf_op | source)
XLA Modules:
  0.0 204.0 jit_solution(16912763031052419279)
XLA Ops:
  7.4 0.0 copy-start
  7.4 0.0 copy-start.2
  7.4 0.0 reduce-scatter.2.cloned.1.call-start
  7.4 3.3 %copy.8 = bf16[128,8192]{0,1:T(8,128)(2,1)S(1)} copy(bf16[128,8192]{1,0:T(8,128)(2,1)} %param.7) | data formatting | bytes 4194304 | tf_op args[0]
  10.7 1.1 fusion.7
  11.8 0.0 copy-done.2
  11.8 3.5 %fusion.9 = bf16[128,8192]{0,1:T(8,128)(2,1)S(1)} fusion(bf16[128,8192]{0,1:T(8,128)(2,1)S(1)} %copy.8, f32[8192]{0:T(1024)S(1)} %copy-done.2, f32[128]{0:T(128)S(1)} %add_rsqrt_fusion), kind=kLoop, calls=%fused_computation.9 | loop fusion | flops 4194304 | bytes 4227584 | tf_op jit(solution)/shard_map/convert_element_type | solution.py:12
  15.3 54.3 %all_to_all.19 = bf16[128,4,2048]{0,2,1:T(8,128)(2,1)S(1)} all-to-all(bf16[128,4,2048]{0,2,1:T(8,128)(2,1)S(1)} %bitcast.19), channel_id=1, replica_groups=mesh['query'=4,'train'=4,'mp'=2] {'train'}, dimensions={1} | all-to-all | bytes 4194304 | tf_op jit(solution)/shard_map/all_to_all | solution.py:15
  69.6 2.7 %copy.9 = bf16[4,128,2048]{2,1,0:T(8,128)(2,1)} copy(bf16[4,128,2048]{1,2,0:T(8,128)(2,1)S(1)} %bitcast.20) | data formatting | bytes 4194304 | tf_op jit(solution)/shard_map/all_to_all | solution.py:15
  72.3 15.3 %fusion.4 = bf16[512,3584]{1,0:T(8,128)(2,1)} fusion(bf16[512,2048]{1,0:T(8,128)(2,1)} %bitcast.21, bf16[2048,1792]{1,0:T(8,128)(2,1)} %param.10, bf16[2048,1792]{1,0:T(8,128)(2,1)} %param.9), kind=kOutput, calls=%fused_computation.4 | convolution fusion | flops 7547387904 | bytes 20447232 | tf_op jit(solution)/shard_map/dot_general | solution.py:18
  87.6 0.0 reduce-scatter.2.cloned.1.call-update
  87.7 0.0 copy-start.1
  87.7 0.0 all-gather.5.cloned.1.call-start
  87.7 0.5 all-gather.5.cloned.1.call-update
  88.3 0.0 all-gather.3.cloned.1.call-start
  88.3 67.3 %reduce-scatter.2.cloned.1.call-done = bf16[128,3584]{1,0:T(8,128)(2,1)} async-done(((bf16[512,3584]{1,0:T(8,128)(2,1)}), bf16[128,3584]{1,0:T(8,128)(2,1)}) %reduce-scatter.2.cloned.1.call-update) | async-done | bytes 917520 | tf_op jit(solution)/shard_map/reduce_scatter | solution.py:17
  155.6 1.4 convert_element_type.18
  157.0 1.0 fusion.12
  158.0 0.0 all-gather.3.cloned.1.call-update
  158.0 0.0 all-gather.5.cloned.1.call-done
  158.1 0.0 copy-done.1
  158.1 2.4 %fusion.14 = f32[32,128]{1,0:T(8,128)S(1)} fusion(bf16[128,8192]{1,0:T(8,128)(2,1)} %all-gather.5.cloned.1.call-done, bf16[1,32,8192]{2,1,0:T(8,128)(2,1)S(1)} %copy-done.1), kind=kOutput, calls=%fused_computation.16 | convolution fusion | flops 67108864 | bytes 2637824 | tf_op jit(solution)/shard_map/dot_general | solution.py:39
  160.5 32.2 %all-gather.3.cloned.1.call-done = bf16[128,14336]{1,0:T(8,128)(2,1)} async-done(((bf16[128,1792]{1,0:T(8,128)(2,1)}), bf16[128,14336]{1,0:T(8,128)(2,1)}) %all-gather.3.cloned.1.call-update) | async-done | bytes 3670032 | tf_op jit(solution)/shard_map/all_gather | solution.py:33
  192.6 0.0 copy-done
  192.7 3.9 %fusion.11 = f32[128]{0:T(128)} fusion(f32[32,128]{1,0:T(8,128)S(1)} %fusion.14, bf16[128,14336]{1,0:T(8,128)(2,1)} %all-gather.3.cloned.1.call-done, bf16[1,32,14336]{2,1,0:T(8,128)(2,1)S(1)} %copy-done), kind=kOutput, calls=%fused_computation.12 | convolution fusion | flops 117448576 | bytes 4604416 | tf_op jit(solution)/shard_map/dot_general | solution.py:31
  (1 shorter events, 0.0 us)
Async XLA Ops:
  7.4 185.3 %copy-start = (bf16[1,32,14336]{2,1,0:T(8,128)(2,1)S(1)}, bf16[1,32,14336]{2,1,0:T(8,128)(2,1)}, u32[]{:S(2)}) copy-start(bf16[1,32,14336]{2,1,0:T(8,128)(2,1)} %param.12) | copy-start | bytes 2752516
  7.4 4.4 %copy-start.2 = (f32[8192]{0:T(1024)S(1)}, f32[8192]{0:T(1024)}, u32[]{:S(2)}) copy-start(f32[8192]{0:T(1024)} %param.8) | copy-start | bytes 98308
  7.4 148.2 %reduce-scatter.2.cloned.1.call-start = ((), (), s32[]{:S(2)}) async-start(), calls=%async_computation.2 | async-start | bytes 4587520 | tf_op jit(solution)/shard_map/reduce_scatter | solution.py:17
  87.7 70.4 %copy-start.1 = (bf16[1,32,8192]{2,1,0:T(8,128)(2,1)S(1)}, bf16[1,32,8192]{2,1,0:T(8,128)(2,1)}, u32[]{:S(2)}) copy-start(bf16[1,32,8192]{2,1,0:T(8,128)(2,1)} %param.13) | copy-start | bytes 1572868
  87.7 70.4 %all-gather.5.cloned.1.call-start = ((), (), s32[]{:S(2)}) async-start(), calls=%async_computation.4 | async-start | bytes 2359296 | tf_op jit(solution)/shard_map/all_gather | solution.py:41
  88.3 104.4 %all-gather.3.cloned.1.call-start = ((), (), s32[]{:S(2)}) async-start(), calls=%async_computation.3 | async-start | bytes 4128768 | tf_op jit(solution)/shard_map/all_gather | solution.py:33
Sparse Core Ops, SparseCore 0:
  87.8 67.7 reduce-scatter.1
Sparse Core Ops, SparseCore 1:
  90.1 26.9 all-gather.4
  158.1 34.5 all-gather.2
where the time goes:
time: 204 us
  waiting for transfers between devices  100 us (49%)
  blocking collectives  54.3 us (27%)
  matrix products  21.6 us (11%)
  between operations  14.9 us (7%)
  other arithmetic  6.99 us (3%)
  local copies, waits for them, and re-layouts  6 us (3%)
    reduce_scatter x1, waiting for transfers between devices, on_device(): lax.psum_scatter(jnp.dot(all_rows, paired, preferred_element_type=jnp.flo...  67.3 us
    all_to_all x1, blocking collectives, on_device(): lax.all_to_all(normed, 'train', split_axis=1, concat_axis=0, tiled=True)  54.3 us
    all_gather x1, waiting for transfers between devices, on_device(): lax.all_gather(activation, ('query', 'mp'), axis=1, tiled=True)  32.2 us
    dot_general x1, matrix products, on_device(): jnp.dot(all_rows, paired, preferred_element_type=jnp.float32)  15.3 us
  transfers between devices with their start and end apart: 3, of which 2 were waited for; matrix products, arithmetic and copies ran while one was open for 2% of the time, Pallas kernels for 0%

commit v1 on v0

--- a/solution.py
+++ b/solution.py
@@ -1,6 +1,10 @@
+import functools
+
 import jax
 import jax.numpy as jnp
 from jax import lax
+from jax.experimental import pallas as pl
+from jax.experimental.pallas import tpu as pltpu
 from jax.sharding import PartitionSpec as P
 
 norm_eps = 1e-05
@@ -45,6 +49,412 @@
     return jnp.sum((projected * sensed).reshape(queries, factor_rank, tok_rows), axis=1)
 
 
+LANES = 128
+SUBLANES = 16
+LAG = 2
+MESH = pl.DeviceIdType.MESH
+NT = (((1,), (1,)), ((), ()))
+
+
+def remote(src, dst, send_sem, recv_sem, device):
+    return pltpu.make_async_remote_copy(
+        src_ref=src,
+        dst_ref=dst,
+        send_sem=send_sem,
+        recv_sem=recv_sem,
+        device_id=device,
+        device_id_type=MESH,
+    )
+
+
+def kernel(
+    n, nq, nm,
+    residual, gain, gate, up, grad, left, right,
+    out,
+    raw, x, w, own, gain_v, stat_own, stat, part, from_up, from_down, lf, rf, grad_v, act,
+    sens_part, sens_in, proj_part, proj_in,
+    ld_sem, w_sem, x_send, x_recv, f_send, f_recv, sib_send, sib_recv,
+    l_send, l_recv, r_send, r_recv, s_send, s_recv, p_send, p_recv, t_send, t_recv,
+    dn_send, dn_recv, up_send, up_recv,
+):
+    q, z, m = lax.axis_index("query"), lax.axis_index("train"), lax.axis_index("mp")
+    planes = nq * nm
+    p = q * nm + m
+    rows = residual.shape[0]
+    depth = gate.shape[0]
+    cols = gate.shape[1]
+    width = grad.shape[1]
+    rank = left.shape[0]
+    chunks = cols // LANES
+    part_rows = rows // planes
+    half = n // 2
+    side = half * rows
+    low = z < half
+    end = jnp.where(low, 0, n - 1)
+    slot = z - jnp.where(low, 0, half)
+    is_end = jnp.logical_or(z == 0, z == n - 1)
+
+    def dev(qq, zz, mm):
+        return {"query": qq, "train": zz, "mp": mm}
+
+    sibling = dev(q, z, 1 - m)
+
+    def piece(zz, qq, mm):
+        start = zz * rows + (qq * nm + mm) * part_rows
+        return raw.at[pl.ds(pl.multiple_of(start, part_rows), part_rows), :]
+
+    def around(d):
+        return lax.rem(z + d, n)
+
+    def x_copy(d):
+        zt = around(d)
+        return remote(
+            residual.at[
+                pl.ds(pl.multiple_of(p * part_rows, part_rows), part_rows),
+                pl.ds(pl.multiple_of(zt * depth, depth), depth),
+            ],
+            piece(z, q, m), x_send.at[d], x_recv.at[z], dev(q, zt, m),
+        )
+
+    for d in range(1, n):
+        x_copy(d).start()
+    own_x = pltpu.make_async_copy(
+        residual.at[:, pl.ds(pl.multiple_of(z * depth, depth), depth)],
+        raw.at[pl.ds(pl.multiple_of(z * rows, rows), rows), :], ld_sem.at[0])
+    own_all = pltpu.make_async_copy(residual, own, ld_sem.at[1])
+    gain_copy = pltpu.make_async_copy(gain, gain_v, ld_sem.at[2])
+    grad_copy = pltpu.make_async_copy(grad, grad_v, ld_sem.at[3])
+
+    def slice_of(factor, span, to):
+        return factor.at[:, pl.ds(pl.multiple_of(to * span, LANES), span)]
+
+    def rows_of(ref, who):
+        return ref.at[pl.ds(pl.multiple_of(who * rank, rank), rank), :]
+
+    own_l = pltpu.make_async_copy(slice_of(left, cols, p), rows_of(lf, p), ld_sem.at[4])
+    own_r = pltpu.make_async_copy(slice_of(right, width, p), rows_of(rf, p), ld_sem.at[5])
+    for copy in (own_all, own_x, gain_copy, grad_copy, own_l, own_r):
+        copy.start()
+
+    def w_copies(c):
+        at = pl.ds(pl.multiple_of(c * LANES, LANES), LANES)
+        return (
+            pltpu.make_async_copy(gate.at[:, at], w.at[c, :, pl.ds(0, LANES)], w_sem.at[c, 0]),
+            pltpu.make_async_copy(up.at[:, at], w.at[c, :, pl.ds(LANES, LANES)], w_sem.at[c, 1]),
+        )
+
+    @pl.loop(0, chunks)
+    def _(c):
+        for copy in w_copies(c):
+            copy.start()
+
+    own_all.wait()
+
+    @pl.loop(0, rows // SUBLANES)
+    def _(i):
+        at = pl.ds(pl.multiple_of(i * SUBLANES, SUBLANES), SUBLANES)
+        v = own[at, :].astype(jnp.float32)
+        mean_sq = jnp.mean(v * v, axis=1, keepdims=True)
+        stat_own[at, :] = jnp.broadcast_to(lax.rsqrt(mean_sq + norm_eps), (SUBLANES, LANES))
+
+    def stat_rows(s):
+        return pl.ds(pl.multiple_of(s * rows, rows), rows)
+
+    stat_copy = remote(
+        stat_own, stat.at[stat_rows(slot), :], t_send.at[0], t_recv.at[slot], dev(q, end, m))
+
+    @pl.when(is_end)
+    def _():
+        stat[stat_rows(slot), :] = stat_own[...]
+
+    @pl.when(jnp.logical_not(is_end))
+    def _():
+        stat_copy.start()
+
+    def spread(d, dq):
+        zs = around(d)
+        if dq == 0:
+            return remote(piece(zs, q, m), piece(zs, q, m), sib_send.at[d, 0], sib_recv.at[zs, q], sibling)
+        return remote(
+            piece(zs, q, m), piece(zs, q, m), f_send.at[d, dq], f_recv.at[zs, q],
+            dev(lax.rem(q + dq, nq), z, m))
+
+    def relay(d, dq):
+        zs, qs = around(d), lax.rem(q + dq, nq)
+        return remote(
+            piece(zs, qs, m), piece(zs, qs, m), sib_send.at[d, dq], sib_recv.at[zs, qs], sibling)
+
+    for d in range(1, n):
+        zs = around(d)
+        remote(piece(zs, q, m), piece(zs, q, m), x_send.at[d], x_recv.at[zs], sibling).wait_recv()
+        for dq in range(nq):
+            spread(d, (dq + 1) % nq).start()
+
+    def factor_copies(k):
+        to = lax.rem(p + k, planes)
+        device = dev(to // nm, z, lax.rem(to, nm))
+        return (
+            remote(slice_of(right, width, to), rows_of(rf, p), r_send.at[k], r_recv.at[p], device),
+            remote(slice_of(left, cols, to), rows_of(lf, p), l_send.at[k], l_recv.at[p], device),
+        )
+
+    for which in range(2):
+        for k in range(1, planes):
+            factor_copies(k)[which].start()
+    for d in range(1, n):
+        zs = around(d)
+        for dq in range(1, nq):
+            qs = lax.rem(q + dq, nq)
+            remote(piece(zs, qs, m), piece(zs, qs, m), f_send.at[d, dq], f_recv.at[zs, qs], sibling).wait_recv()
+            relay(d, dq).start()
+    own_x.wait()
+    gain_copy.wait()
+    for d in range(1, n):
+        zs = around(d)
+        for dq in range(nq):
+            qs = lax.rem(q + dq, nq)
+            at = piece(zs, qs, 1 - m)
+            remote(at, at, sib_send.at[d, dq], sib_recv.at[zs, qs], sibling).wait_recv()
+
+    @pl.loop(0, n * rows // (4 * SUBLANES))
+    def _(i):
+        at = pl.ds(pl.multiple_of(i * 4 * SUBLANES, 4 * SUBLANES), 4 * SUBLANES)
+        g = gain_v[:, pl.ds(pl.multiple_of(z * depth, depth), depth)]
+        x[at, :] = (raw[at, :].astype(jnp.float32) * g).astype(jnp.bfloat16)
+
+    down_rows, up_rows = pl.ds(0, side), pl.ds(side, side)
+
+    def down_copy(c):
+        return remote(
+            part.at[c, down_rows, :], from_up.at[c], dn_send.at[c], dn_recv.at[c],
+            dev(q, jnp.maximum(z - 1, 0), m))
+
+    def up_copy(c):
+        return remote(
+            part.at[c, up_rows, :], from_down.at[c], up_send.at[c], up_recv.at[c],
+            dev(q, jnp.minimum(z + 1, n - 1), m))
+
+    for s in range(half):
+        arrives = jnp.logical_and(is_end, slot != s)
+
+        @pl.when(arrives)
+        def _():
+            remote(stat_own, stat.at[stat_rows(s), :], t_send.at[0], t_recv.at[s], sibling).wait_recv()
+
+    def finish(c, total):
+        s = stat[:, 0:1]
+        g = total[:, :LANES] * s
+        u = total[:, LANES:] * s
+        act[:, pl.ds(pl.multiple_of(c * LANES, LANES), LANES)] = (
+            g / (1.0 + jnp.exp(-g)) * u).astype(jnp.bfloat16)
+
+    def pass_on(i, hops, arrived, copy, keep, last):
+        c = i - LAG * hops
+
+        @pl.when(jnp.logical_and(hops > 0, jnp.logical_and(c >= 0, c < chunks)))
+        def _():
+            copy(c).wait_recv()
+
+            @pl.when(last)
+            def _():
+                finish(c, part[c, keep, :].astype(jnp.float32) + arrived[c].astype(jnp.float32))
+
+            @pl.when(jnp.logical_not(last))
+            def _():
+                part[c, keep, :] = (
+                    part[c, keep, :].astype(jnp.float32) + arrived[c].astype(jnp.float32)
+                ).astype(jnp.bfloat16)
+                copy(c).start()
+
+    def sens_copy(k):
+        to = lax.rem(p + k, planes)
+        return remote(
+            sens_part.at[to], sens_in.at[p], s_send.at[k], s_recv.at[p],
+            dev(to // nm, z, lax.rem(to, nm)))
+
+    def step(i, carry):
+        @pl.when(i < chunks)
+        def _():
+            for copy in w_copies(i):
+                copy.wait()
+            part[i] = jnp.dot(x[...], w[i], preferred_element_type=jnp.float32).astype(jnp.bfloat16)
+
+            @pl.when(z == n - 1)
+            def _():
+                down_copy(i).start()
+
+            @pl.when(z == 0)
+            def _():
+                up_copy(i).start()
+
+        pass_on(i, n - 1 - z, from_up, down_copy, down_rows, z == 0)
+        pass_on(i, z, from_down, up_copy, up_rows, z == n - 1)
+
+        @pl.when(i == chunks)
+        def _():
+            own_r.wait()
+            grad_copy.wait()
+            for k in range(1, planes):
+                who = lax.rem(p + k, planes)
+                at = rows_of(rf, who)
+                remote(at, at, r_send.at[k], r_recv.at[who], sibling).wait_recv()
+            sens_part[...] = lax.dot_general(
+                rf[...], grad_v[...], NT, preferred_element_type=jnp.float32
+            ).reshape(planes, rank, rows)
+            sens_in[p] = sens_part[p]
+            for k in range(1, planes):
+                sens_copy(k).start()
+
+        return carry
+
+    lax.fori_loop(0, chunks + LAG * (n - 1), step, 0)
+
+    own_l.wait()
+    for k in range(1, planes):
+        who = lax.rem(p + k, planes)
+        at = rows_of(lf, who)
+        remote(at, at, l_send.at[k], l_recv.at[who], sibling).wait_recv()
+
+    def proj_copy(s, k):
+        to = lax.rem(p + k, planes)
+        return remote(
+            proj_part.at[s, to], proj_in.at[p], p_send.at[s, k], p_recv.at[p],
+            dev(to // nm, jnp.where(low, 0, half) + s, lax.rem(to, nm)))
+
+    @pl.when(is_end)
+    def _():
+        product = lax.dot_general(lf[...], act[...], NT, preferred_element_type=jnp.float32)
+        for s in range(half):
+            proj_part[s] = product[:, s * rows:(s + 1) * rows].reshape(planes, rank, rows)
+        for s in range(half):
+            for k in range(planes):
+                if k > 0:
+                    proj_copy(s, k).start()
+                else:
+                    @pl.when(slot == s)
+                    def _():
+                        proj_in[p] = proj_part[s, p]
+
+                    @pl.when(slot != s)
+                    def _():
+                        proj_copy(s, k).start()
+
+    for k in range(1, planes):
+        who = lax.rem(p + k, planes)
+        remote(sens_part.at[0], sens_in.at[who], s_send.at[k], s_recv.at[who], sibling).wait_recv()
+    for k in range(1, planes):
+        who = lax.rem(p + k, planes)
+        remote(proj_part.at[0, 0], proj_in.at[who], p_send.at[0, k], p_recv.at[who], sibling).wait_recv()
+
+    @pl.when(jnp.logical_not(is_end))
+    def _():
+        remote(proj_part.at[0, 0], proj_in.at[p], p_send.at[0, 0], p_recv.at[p], sibling).wait_recv()
+
+    projected = jnp.sum(proj_in[...], axis=0)
+    sensed = jnp.sum(sens_in[...], axis=0)
+    out[...] = jnp.sum(projected * sensed, axis=0, keepdims=True)
+
+    for d in range(1, n):
+        x_copy(d).wait_send()
+        for dq in range(nq):
+            spread(d, dq).wait_send()
+        for dq in range(1, nq):
+            relay(d, dq).wait_send()
+    for k in range(1, planes):
+        for copy in factor_copies(k):
+            copy.wait_send()
+        sens_copy(k).wait_send()
+
+    @pl.when(jnp.logical_not(is_end))
+    def _():
+        stat_copy.wait_send()
+
+    @pl.when(z > 0)
+    def _():
+        @pl.loop(0, chunks)
+        def _(c):
+            down_copy(c).wait_send()
+
+    @pl.when(z < n - 1)
+    def _():
+        @pl.loop(0, chunks)
+        def _(c):
+            up_copy(c).wait_send()
+
+    @pl.when(is_end)
+    def _():
+        for s in range(half):
+            for k in range(planes):
+                if k > 0:
+                    proj_copy(s, k).wait_send()
+                else:
+                    @pl.when(slot != s)
+                    def _():
+                        proj_copy(s, k).wait_send()
+
+
+def in_one_kernel(n, nq, nm, residual, norm_gain, gate_weight, up_weight, out_grad, left_factor, right_factor):
+    rows, features = residual.shape
+    depth, cols = gate_weight.shape
+    width = out_grad.shape[1]
+    rank = left_factor.shape[1]
+    planes = nq * nm
+    chunks, half = cols // LANES, n // 2
+    bf16, f32 = jnp.bfloat16, jnp.float32
+    dma = pltpu.SemaphoreType.DMA
+    return pl.pallas_call(
+        functools.partial(kernel, n, nq, nm),
+        out_shape=jax.ShapeDtypeStruct((1, rows), f32),
+        in_specs=[pl.BlockSpec(memory_space=pl.ANY)] * 7,
+        out_specs=pl.BlockSpec(memory_space=pltpu.VMEM),
+        scratch_shapes=[
+            pltpu.VMEM((n * rows, depth), bf16),
+            pltpu.VMEM((n * rows, depth), bf16),
+            pltpu.VMEM((chunks, depth, 2 * LANES), bf16),
+            pltpu.VMEM((rows, features), bf16),
+            pltpu.VMEM((1, features), f32),
+            pltpu.VMEM((rows, LANES), f32),
+            pltpu.VMEM((half * rows, LANES), f32),
+            pltpu.VMEM((chunks, n * rows, 2 * LANES), bf16),
+            pltpu.VMEM((chunks, half * rows, 2 * LANES), bf16),
+            pltpu.VMEM((chunks, half * rows, 2 * LANES), bf16),
+            pltpu.VMEM((planes * rank, cols), bf16),
+            pltpu.VMEM((planes * rank, width), bf16),
+            pltpu.VMEM((rows, width), bf16),
+            pltpu.VMEM((half * rows, cols), bf16),
+            pltpu.VMEM((planes, rank, rows), f32),
+            pltpu.VMEM((planes, rank, rows), f32),
+            pltpu.VMEM((half, planes, rank, rows), f32),
+            pltpu.VMEM((planes, rank, rows), f32),
+            dma((6,)), dma((chunks, 2)), dma((n,)), dma((n,)),
+            dma((n, nq)), dma((n, nq)), dma((n, nq)), dma((n, nq)),
+            dma((planes,)), dma((planes,)), dma((planes,)), dma((planes,)),
+            dma((planes,)), dma((planes,)), dma((half, planes)), dma((planes,)),
+            dma((1,)), dma((half,)),
+            dma((chunks,)), dma((chunks,)), dma((chunks,)), dma((chunks,)),
+        ],
+        compiler_params=pltpu.CompilerParams(has_side_effects=True, vmem_limit_bytes=60 * 2**20),
+    )(
+        residual, norm_gain[None, :], gate_weight, up_weight, out_grad,
+        left_factor.reshape(rank, -1), right_factor.reshape(rank, -1),
+    )
+
+
+def fits(n, nq, nm, residual, gate_weight, out_grad, left_factor):
+    rows = residual.shape[0]
+    return (
+        n % 2 == 0
+        and nm == 2
+        and rows % LANES == 0
+        and rows % (nq * nm * SUBLANES) == 0
+        and gate_weight.shape[0] % LANES == 0
+        and gate_weight.shape[1] % LANES == 0
+        and out_grad.shape[1] % LANES == 0
+        and left_factor.shape[0] == 1
+        and left_factor.shape[1] % SUBLANES == 0
+    )
+
+
 def solution(mesh):
     placed = (
         P("train", None),
@@ -55,8 +465,16 @@
         P(("query", "mp"), None, None),
         P(("query", "mp"), None, None),
     )
+    n, nq, nm = (mesh.shape[axis] for axis in ("train", "query", "mp"))
+
+    def chosen(residual, norm_gain, gate_weight, up_weight, out_grad, left_factor, right_factor):
+        args = (residual, norm_gain, gate_weight, up_weight, out_grad, left_factor, right_factor)
+        if fits(n, nq, nm, residual, gate_weight, out_grad, left_factor):
+            return in_one_kernel(n, nq, nm, *args)
+        return on_device(*args)
+
     return jax.shard_map(
-        on_device,
+        chosen,
         mesh=mesh,
         in_specs=placed,
         out_specs=P(("query", "mp"), "train"),

time: 204 us -> 88.9 us (0.44)
  waiting for transfers between devices: 100 us -> 0 us
  Pallas kernels: 0 us -> 87.6 us
  blocking collectives: 54.3 us -> 0 us
  matrix products: 21.6 us -> 0 us
  between operations: 14.9 us -> 0.01 us
  other arithmetic: 6.99 us -> 0 us
  local copies, waits for them, and re-layouts: 6 us -> 1.19 us
    pallas_call x0 -> x1, Pallas kernels: none -> 87.6 us  [in_one_kernel(): pl.pallas_call(functools.partial(kernel, n, nq, nm), out_shape=jax.ShapeD...]
    reduce_scatter x1 -> x0, waiting for transfers between devices: 67.3 us -> none  [on_device(): lax.psum_scatter(jnp.dot(all_rows, paired, preferred_element_type=jnp.flo...]
    all_to_all x1 -> x0, blocking collectives: 54.3 us -> none  [on_device(): lax.all_to_all(normed, 'train', split_axis=1, concat_axis=0, tiled=True)]
    all_gather x2 -> x0, waiting for transfers between devices: 32.2 us -> none  [the longest x1 32.2 us: on_device(): lax.all_gather(activation, ('query', 'mp'), axis=1, tiled=True)]
    dot_general x3 -> x0, matrix products: 21.6 us -> none  [the longest x1 15.3 us: on_device(): jnp.dot(all_rows, paired, preferred_element_type=jnp.float32)]
    convert_element_type x3 -> x0, other arithmetic: 5.88 us -> none  [the longest x1 3.49 us: on_device(): (values * lax.rsqrt(mean_sq + norm_eps) * norm_gain[None, :]).astype(jnp....]
    all_to_all x1 -> x0, local copies, waits for them, and re-layouts: 2.68 us -> none  [on_device(): lax.all_to_all(normed, 'train', split_axis=1, concat_axis=0, tiled=True)]
    unnamed x7 -> x1, local copies, waits for them, and re-layouts: 3.32 us -> 1.19 us
  transfers between devices with their start and end apart: 3 -> 0, of which waited for: 2 -> 0; matrix products, arithmetic and copies ran while one was open for 2% -> 0% of each run, Pallas kernels for 0% -> 0%
where the time goes in v1:
time: 88.9 us; the launch traced here: 88.8 us
  Pallas kernels  87.6 us (99%)
  local copies, waits for them, and re-layouts  1.19 us (1%)
    pallas_call x1, Pallas kernels, in_one_kernel(): pl.pallas_call(functools.partial(kernel, n, nq, nm), out_shape=jax.ShapeD...  87.6 us

profile of v1, /device:TPU:0, one launch (start us, length us, event | category | flops | bytes accessed | tf_op | source)
XLA Modules:
  0.0 88.8 jit_solution(13032756011433411334)
XLA Ops:
  0.0 87.6 %shard_map.73 = f32[1,128]{1,0:T(1,128)} custom-call(bf16[128,8192]{1,0:T(8,128)(2,1)} %residual.1, f32[1,8192]{1,0:T(1,128)} %bitcast.5, bf16[2048,1792]{1,0:T(8,128)(2,1)} %gate.1, bf16[2048,1792]{1,0:T(8,128)(2,1)} %up.1, bf16[128,1024]{1,0:T(8,128)(2,1)} %grad.1, bf16[32,14336]{1,0:T(8,128)(2,1)} %bitcast.3, bf16[32,8192]{1,0:T(8,128)(2,1)} %bitcast.4), custom_call_target="tpu_custom_call" | custom-call | tf_op jit(solution)/shard_map/pallas_call | solution.py:405
  87.6 1.2 %copy.9 = f32[1,128]{1,0:T(1,128)} copy(f32[1,128]{1,0:T(1,128)} %shard_map.73) | data formatting | bytes 1024

commit v2 on v1

--- a/solution.py
+++ b/solution.py
@@ -98,6 +98,22 @@
         return {"query": qq, "train": zz, "mp": mm}
 
     sibling = dev(q, z, 1 - m)
+    base, other = jnp.where(low, 0, half), jnp.where(low, half, 0)
+    barrier = pltpu.get_barrier_semaphore()
+
+    def greet(device):
+        pl.semaphore_signal(barrier, inc=1, device_id=device, device_id_type=MESH)
+
+    for s in range(half):
+        greet(dev(q, other + s, m))
+        for k in range(planes):
+            to = lax.rem(p + k, planes)
+            if k > 0:
+                greet(dev(to // nm, base + s, lax.rem(to, nm)))
+            else:
+                @pl.when(slot != s)
+                def _():
+                    greet(dev(q, base + s, m))
 
     def piece(zz, qq, mm):
         start = zz * rows + (qq * nm + mm) * part_rows
@@ -116,8 +132,6 @@
             piece(z, q, m), x_send.at[d], x_recv.at[z], dev(q, zt, m),
         )
 
-    for d in range(1, n):
-        x_copy(d).start()
     own_x = pltpu.make_async_copy(
         residual.at[:, pl.ds(pl.multiple_of(z * depth, depth), depth)],
         raw.at[pl.ds(pl.multiple_of(z * rows, rows), rows), :], ld_sem.at[0])
@@ -133,7 +147,12 @@
 
     own_l = pltpu.make_async_copy(slice_of(left, cols, p), rows_of(lf, p), ld_sem.at[4])
     own_r = pltpu.make_async_copy(slice_of(right, width, p), rows_of(rf, p), ld_sem.at[5])
-    for copy in (own_all, own_x, gain_copy, grad_copy, own_l, own_r):
+    for copy in (own_all, own_x, gain_copy):
+        copy.start()
+    pl.semaphore_wait(barrier, half * planes - 1 + half)
+    for d in range(1, n):
+        x_copy(d).start()
+    for copy in (grad_copy, own_r, own_l):
         copy.start()
 
     def w_copies(c):
@@ -190,23 +209,22 @@
         for dq in range(nq):
             spread(d, (dq + 1) % nq).start()
 
-    def factor_copies(k):
+    def factor_copy(k, which):
         to = lax.rem(p + k, planes)
         device = dev(to // nm, z, lax.rem(to, nm))
-        return (
-            remote(slice_of(right, width, to), rows_of(rf, p), r_send.at[k], r_recv.at[p], device),
-            remote(slice_of(left, cols, to), rows_of(lf, p), l_send.at[k], l_recv.at[p], device),
-        )
-
-    for which in range(2):
-        for k in range(1, planes):
-            factor_copies(k)[which].start()
+        if which == 0:
+            return remote(slice_of(right, width, to), rows_of(rf, p), r_send.at[k], r_recv.at[p], device)
+        return remote(slice_of(left, cols, to), rows_of(lf, p), l_send.at[k], l_recv.at[p], device)
+
     for d in range(1, n):
         zs = around(d)
         for dq in range(1, nq):
             qs = lax.rem(q + dq, nq)
             remote(piece(zs, qs, m), piece(zs, qs, m), f_send.at[d, dq], f_recv.at[zs, qs], sibling).wait_recv()
             relay(d, dq).start()
+    for which in range(2):
+        for k in range(1, planes):
+            factor_copy(k, which).start()
     own_x.wait()
     gain_copy.wait()
     for d in range(1, n):
@@ -361,8 +379,8 @@
         for dq in range(1, nq):
             relay(d, dq).wait_send()
     for k in range(1, planes):
-        for copy in factor_copies(k):
-            copy.wait_send()
+        for which in range(2):
+            factor_copy(k, which).wait_send()
         sens_copy(k).wait_send()
 
     @pl.when(jnp.logical_not(is_end))
@@ -433,7 +451,7 @@
             dma((1,)), dma((half,)),
             dma((chunks,)), dma((chunks,)), dma((chunks,)), dma((chunks,)),
         ],
-        compiler_params=pltpu.CompilerParams(has_side_effects=True, vmem_limit_bytes=60 * 2**20),
+        compiler_params=pltpu.CompilerParams(collective_id=0, has_side_effects=True, vmem_limit_bytes=60 * 2**20),
     )(
         residual, norm_gain[None, :], gate_weight, up_weight, out_grad,
         left_factor.reshape(rank, -1), right_factor.reshape(rank, -1),

time: 88.9 us -> 82.9 us (0.933)
  Pallas kernels: 87.6 us -> 81.5 us
    pallas_call x1, Pallas kernels: 87.6 us -> 81.5 us  [in_one_kernel(): pl.pallas_call(functools.partial(kernel, n, nq, nm), out_shape=jax.ShapeD...]
where the time goes in v2:
time: 82.9 us; the launch traced here: 82.7 us
  Pallas kernels  81.5 us (98%)
  local copies, waits for them, and re-layouts  1.19 us (1%)
    pallas_call x1, Pallas kernels, in_one_kernel(): pl.pallas_call(functools.partial(kernel, n, nq, nm), out_shape=jax.ShapeD...  81.5 us

profile of v2, /device:TPU:0, one launch (start us, length us, event | category | flops | bytes accessed | tf_op | source)
XLA Modules:
  0.0 82.7 jit_solution(5294090210813869091)
XLA Ops:
  0.0 81.5 %shard_map.73 = f32[1,128]{1,0:T(1,128)} custom-call(bf16[128,8192]{1,0:T(8,128)(2,1)} %residual.1, f32[1,8192]{1,0:T(1,128)} %bitcast.5, bf16[2048,1792]{1,0:T(8,128)(2,1)} %gate.1, bf16[2048,1792]{1,0:T(8,128)(2,1)} %up.1, bf16[128,1024]{1,0:T(8,128)(2,1)} %grad.1, bf16[32,14336]{1,0:T(8,128)(2,1)} %bitcast.3, bf16[32,8192]{1,0:T(8,128)(2,1)} %bitcast.4), custom_call_target="tpu_custom_call" | custom-call | tf_op jit(solution)/shard_map/pallas_call | solution.py:423
  81.5 1.2 %copy.9 = f32[1,128]{1,0:T(1,128)} copy(f32[1,128]{1,0:T(1,128)} %shard_map.73) | data formatting | bytes 1024
